TPU v7x, 32 devices: a whole 2x2x4 slice. The times are simulated.
32 devices in a mesh: fsdp: 16 (over z, y, x), dp: 2 (over core).
Axes of the slice: x: 2, y: 2, z: 4, core: 2. Of those that a mesh axis runs over, the one named last changes fastest.
Arguments:
- gradients: bfloat16 [2, 64, 256, 256], P('dp', 'fsdp'), may hold values from -6 to 6
- first_moment: float32 [96, 256, 256], P('fsdp'), may hold values from -4 to 4
- second_moment: float32 [96, 256, 256], P('fsdp'), may hold values from 0.05 to 2
- left_basis: float32 [96, 256, 256], P('fsdp'), may hold values from -1 to 1, as said below
- right_basis: float32 [96, 256, 256], P('fsdp'), may hold values from -1 to 1, as said below
- shard_starts: int32 [16], replicated, may hold values from 0 to 48, as said below
- block_owners: int32 [48], replicated, may hold values from 0 to 15, as said below
Outputs:
- direction: float32 [64, 256, 256], P('fsdp')
- first_new: float32 [96, 256, 256], P('fsdp')
- second_new: float32 [96, 256, 256], P('fsdp')
Inputs may be any that keep to these rules, and one draw needn't show every extreme that they name: Starts never fall and shard_starts[0] = 0; a device holds at most 4 blocks, some device exactly 4 and some none. `block_owners`: never falls; a device owns at most 6 blocks, some device exactly 6 and some none; a block's owner differs from its holder by at most 2 fsdp indices, by exactly 2 for some block in each direction. `left_basis`: each matrix is orthogonal up to float32 rounding. `right_basis`: each matrix is orthogonal up to float32 rounding.
All inputs are finite; a program needn't handle non-finite values.
Results may differ from a plain program's by a relative error of at most 0.0014.
Values may be sent and summed in bfloat16 or wider, within the bound.
A program may use at most 64 MiB of HBM per device.

v0:
```python
import jax
import jax.numpy as jnp
from jax import lax
from jax.sharding import PartitionSpec as P

REACH = 2
STEP = 10


beta_one = 0.9
beta_two = 0.95
epsilon = 1e-08


def from_behind(value, axis, steps):
    count = lax.axis_size(axis)
    initial, last = (max(0, -steps), min(count, count - steps))
    return lax.ppermute(value, axis, [(source, source + steps) for source in range(initial, last)])


def soap_blocks(gradient, moment_one, moment_two, left_basis, right_basis):
    highest = lax.Precision.HIGHEST
    moment_new = beta_one * moment_one + (1.0 - beta_one) * gradient
    turned = jnp.einsum(
        "jad,jde->jae",
        jnp.einsum("jba,jbd->jad", left_basis, gradient, precision=highest),
        right_basis,
        precision=highest,
    )
    turned_moment = jnp.einsum(
        "jad,jde->jae",
        jnp.einsum("jba,jbd->jad", left_basis, moment_new, precision=highest),
        right_basis,
        precision=highest,
    )
    second_next = beta_two * moment_two + (1.0 - beta_two) * turned * turned
    bias_one = 1.0 - beta_one**STEP
    bias_two = 1.0 - beta_two**STEP
    scaled = turned_moment / bias_one / (jnp.sqrt(second_next / bias_two) + epsilon)
    update = jnp.einsum(
        "jad,jed->jae",
        jnp.einsum("jab,jbd->jad", left_basis, scaled, precision=highest),
        right_basis,
        precision=highest,
    )
    return (moment_new, second_next, update)


def layout(shard_starts, block_owners, devices):
    total_blocks = block_owners.shape[0]
    ends = jnp.concatenate([shard_starts[1:], jnp.full((1,), total_blocks, jnp.int32)])
    held_counts = ends - shard_starts
    device_ids = jnp.arange(devices, dtype=jnp.int32)
    own_counts = jnp.sum((block_owners[None, :] == device_ids[:, None]).astype(jnp.int32), axis=1)
    firsts = jnp.cumsum(own_counts) - own_counts
    return (held_counts, own_counts, firsts)


def linking(own_first, own_count, hold_start, hold_count, in_range, slot_count, owned_slots):
    owner_pos = own_first + jnp.arange(owned_slots, dtype=jnp.int32)
    holder_pos = hold_start + jnp.arange(slot_count, dtype=jnp.int32)
    live_pair = (
        (jnp.arange(owned_slots)[:, None] < own_count)
        & (jnp.arange(slot_count)[None, :] < hold_count)
        & in_range
    )
    return (owner_pos[:, None] == holder_pos[None, :]) & live_pair


def body(
    gradients, first_moment, second_moment, left_basis, right_basis, shard_starts, block_owners
):
    devices = lax.axis_size("fsdp")
    myself = lax.axis_index("fsdp")
    slot_count = gradients.shape[1]
    owned_slots = first_moment.shape[0]
    block_width = gradients.shape[3]
    held_counts, own_counts, firsts = layout(shard_starts, block_owners, devices)
    summed = lax.psum_scatter(
        gradients[0].astype(jnp.float32).astype(jnp.bfloat16), "dp", scatter_dimension=1, tiled=True
    )
    assembled = jnp.zeros((owned_slots, summed.shape[1], block_width), jnp.float32)
    for offset in range(-REACH, REACH + 1):
        source = myself - offset
        if offset == 0:
            arriving = summed
        else:
            arriving = from_behind(summed, "fsdp", offset)
        in_range = (source >= 0) & (source < devices)
        picked = jnp.clip(source, 0, devices - 1)
        matching = linking(
            firsts[myself],
            own_counts[myself],
            shard_starts[picked],
            held_counts[picked],
            in_range,
            slot_count,
            owned_slots,
        )
        assembled = assembled + jnp.einsum(
            "js,sab->jab",
            matching.astype(jnp.bfloat16),
            arriving,
            preferred_element_type=jnp.float32,
        )
    gradient = lax.all_gather(assembled.astype(jnp.bfloat16), "dp", axis=1, tiled=True).astype(
        jnp.float32
    )
    own_live = own_counts[myself]
    moment_new, second_next, update = soap_blocks(
        gradient, first_moment, second_moment, left_basis, right_basis
    )
    live_slots = (jnp.arange(owned_slots) < own_live)[:, None, None]
    moment_new = jnp.where(live_slots, moment_new, 0.0)
    second_next = jnp.where(live_slots, second_next, 0.0)
    update = jnp.where(live_slots, update, 0.0)
    half_rows = block_width // lax.axis_size("dp")
    sending = lax.dynamic_slice_in_dim(update, lax.axis_index("dp") * half_rows, half_rows, 1)
    collected = jnp.zeros((slot_count, sending.shape[1], block_width), jnp.float32)
    for offset in range(-REACH, REACH + 1):
        source = myself + offset
        if offset == 0:
            arriving = sending
        else:
            arriving = from_behind(sending, "fsdp", -offset)
        in_range = (source >= 0) & (source < devices)
        picked = jnp.clip(source, 0, devices - 1)
        matching = linking(
            firsts[picked],
            own_counts[picked],
            shard_starts[myself],
            held_counts[myself],
            in_range,
            slot_count,
            owned_slots,
        )
        collected = collected + jnp.einsum(
            "js,jab->sab", matching.astype(jnp.float32), arriving, precision=lax.Precision.HIGHEST
        )
    direction = lax.all_gather(collected, "dp", axis=1, tiled=True)
    return (direction, moment_new, second_next)


def solution(mesh):
    in_specs = (
        P("dp", "fsdp", None, None),
        P("fsdp", None, None),
        P("fsdp", None, None),
        P("fsdp", None, None),
        P("fsdp", None, None),
        P(),
        P(),
    )
    out_specs = (P("fsdp", None, None), P("fsdp", None, None), P("fsdp", None, None))
    return jax.shard_map(body, mesh=mesh, in_specs=in_specs, out_specs=out_specs, check_vma=False)
```

profile of v0, /device:TPU:17, one launch (start us, length us, event | category | flops | bytes accessed | tf_op | source)
XLA Modules:
  0.0 160.0 jit_solution(13953221525241802722)
XLA Ops:
  7.3 2.3 %copy.77 = bf16[1,4,256,256]{3,1,2,0:T(4,128)(2,1)} copy(bf16[1,4,256,256]{3,2,1,0:T(8,128)(2,1)} %param.7) | data formatting | bytes 1048576 | tf_op args[0]
  24.4 7.0 %all-reduce.3.cloned.1.call-done = bf16[4,256,256]{2,0,1:T(4,128)(2,1)} async-done(((bf16[4,256,256]{2,0,1:T(4,128)(2,1)}), bf16[4,256,256]{2,0,1:T(4,128)(2,1)}) %all-reduce.3.cloned.1.call-update) | async-done | bytes 524304
  32.4 4.0 %collective-permute-start.1 = (bf16[4,128,256]{2,0,1:T(4,128)(2,1)S(1)}, bf16[4,128,256]{2,0,1:T(4,128)(2,1)S(1)}, u32[]{:S(2)}, u32[]{:S(2)}) collective-permute-start(bf16[4,128,256]{2,0,1:T(4,128)(2,1)S(1)} %constant_dynamic-slice_fusion), channel_id=1, source_target_pairs={{2,0},{4,2},{6,4},{8,6},{10,8},{12,10},{14,12},{16,14},{18,16},{20... | collective-permute-start | bytes 786440 | tf_op jit(solution)/shard_map/ppermute | solution.py:18
  37.1 2.2 %collective-permute-start = (bf16[4,128,256]{2,0,1:T(4,128)(2,1)S(1)}, bf16[4,128,256]{2,0,1:T(4,128)(2,1)S(1)}, u32[]{:S(2)}, u32[]{:S(2)}) collective-permute-start(bf16[4,128,256]{2,0,1:T(4,128)(2,1)S(1)} %constant_dynamic-slice_fusion), channel_id=1, source_target_pairs={{4,0},{6,2},{8,4},{10,6},{12,8},{14,10},{16,12},{18,14},{20,16},{2... | collective-permute-start | bytes 786440 | tf_op jit(solution)/shard_map/ppermute | solution.py:18
  39.2 3.1 %collective-permute-start.3 = (bf16[4,128,256]{2,0,1:T(4,128)(2,1)S(1)}, bf16[4,128,256]{2,0,1:T(4,128)(2,1)S(1)}, u32[]{:S(2)}, u32[]{:S(2)}) collective-permute-start(bf16[4,128,256]{2,0,1:T(4,128)(2,1)S(1)} %constant_dynamic-slice_fusion), channel_id=1, source_target_pairs={{0,4},{2,6},{4,8},{6,10},{8,12},{10,14},{12,16},{14,18},{16,20},{1... | collective-permute-start | bytes 786440 | tf_op jit(solution)/shard_map/ppermute | solution.py:18
  42.4 1.9 %collective-permute-start.2 = (bf16[4,128,256]{2,0,1:T(4,128)(2,1)S(1)}, bf16[4,128,256]{2,0,1:T(4,128)(2,1)S(1)}, u32[]{:S(2)}, u32[]{:S(2)}) collective-permute-start(bf16[4,128,256]{2,0,1:T(4,128)(2,1)S(1)} %constant_dynamic-slice_fusion), channel_id=1, source_target_pairs={{0,2},{2,4},{4,6},{6,8},{8,10},{10,12},{12,14},{14,16},{16,18},{18... | collective-permute-start | bytes 786440 | tf_op jit(solution)/shard_map/ppermute | solution.py:18
  45.1 12.4 %collective-permute-done = bf16[4,128,256]{2,0,1:T(4,128)(2,1)S(1)} collective-permute-done((bf16[4,128,256]{2,0,1:T(4,128)(2,1)S(1)}, bf16[4,128,256]{2,0,1:T(4,128)(2,1)S(1)}, u32[]{:S(2)}, u32[]{:S(2)}) %collective-permute-start) | collective-permute-done | bytes 262176 | tf_op jit(solution)/shard_map/ppermute | solution.py:18
  59.6 3.8 %all_gather.6 = bf16[6,256,256]{2,1,0:T(8,128)(2,1)S(1)} all-gather(bf16[6,128,256]{2,1,0:T(8,128)(2,1)S(1)} %copy.47), channel_id=1, replica_groups=mesh['fsdp'=16,'dp'=2] {'dp'}, dimensions={1}, use_global_device_ids=true | all-gather | bytes 1179648 | tf_op jit(solution)/shard_map/all_gather | solution.py:106
  63.4 1.4 fusion.143
  64.8 2.8 %fusion.21 = f32[6,256,256]{1,2,0:T(8,128)S(1)} fusion(f32[6,256,256]{2,1,0:T(8,128)S(1)} %copy-done.1, bf16[6,256,256]{2,1,0:T(8,128)(2,1)S(1)} %all_gather.6, f32[6,256,256]{2,1,0:T(8,128)S(1)} %copy-done.2), kind=kOutput, calls=%fused_computation.27 | convolution fusion | flops 1209532416 | bytes 5505024 | tf_op jit(solution)/shard_map/jba,jbd->jad/dot_general | solution.py:32
  67.6 1.6 %fusion.142 = f32[6,256,256]{2,1,0:T(8,128)S(1)} fusion(f32[6,256,256]{1,2,0:T(8,128)S(1)} %fusion.21, f32[6,256,256]{2,1,0:T(8,128)S(1)} %copy-done), kind=kOutput, calls=%fused_computation.178 | convolution fusion | flops 1207959552 | bytes 4718592 | tf_op jit(solution)/shard_map/jad,jde->jae/dot_general | solution.py:30
  69.3 3.5 %broadcast_select_fusion = (f32[6,256,256]{2,1,0:T(8,128)}, f32[6,256,256]{2,1,0:T(8,128)}, f32[6,256,256]{2,1,0:T(8,128)S(1)}) fusion(pred[6]{0:T(512)(128)(4,1)S(1)} %iota_compare_fusion.10, f32[6,256,256]{2,1,0:T(8,128)S(1)} %copy-done.3, bf16[6,256,256]{2,1,0:T(8,128)(2,1)S(1)} %all_gather.6, f32[6,256,256]{2,1,0:T(8,128)S(1)} %copy-done.2, ...), kind=kOutput, calls=%fused_computation.29 | convolution fusion | flops 1211891712 | bytes 11796486 | tf_op jit(solution)/shard_map/jad,jde->jae/dot_general | solution.py:24
  72.8 2.7 %fusion.1 = f32[6,256,256]{1,2,0:T(8,128)S(1)} fusion(f32[6,256,256]{2,1,0:T(8,128)S(1)} %copy-done.1, f32[6,256,256]{2,1,0:T(8,128)S(1)} %fusion.142, f32[6,256,256]{2,1,0:T(8,128)S(1)} %get-tuple-element.41, f32[6,256,256]{2,1,0:T(8,128)S(1)} %copy-done.3), kind=kOutput, calls=%fused_computation.2 | convolution fusion | flops 1211105280 | bytes 7864320 | tf_op jit(solution)/shard_map/jab,jbd->jad/dot_general | solution.py:42
  75.5 1.9 %fusion.144 = f32[6,256,256]{2,1,0:T(8,128)S(1)} fusion(f32[6,256,256]{1,2,0:T(8,128)S(1)} %fusion.1, f32[6,256,256]{2,1,0:T(8,128)S(1)} %copy-done), kind=kOutput, calls=%fused_computation.180 | convolution fusion | flops 1207959552 | bytes 4718592 | tf_op jit(solution)/shard_map/jad,jed->jae/dot_general | solution.py:40
  77.6 1.9 %collective-permute-start.5 = (f32[6,128,256]{2,1,0:T(8,128)S(1)}, f32[6,128,256]{2,1,0:T(8,128)S(1)}, u32[]{:S(2)}, u32[]{:S(2)}) collective-permute-start(f32[6,128,256]{2,1,0:T(8,128)S(1)} %dynamic-slice_select_fusion), channel_id=1, source_target_pairs={{0,2},{2,4},{4,6},{6,8},{8,10},{10,12},{12,14},{14,16},{16,18},{18... | collective-permute-start | bytes 2359304 | tf_op jit(solution)/shard_map/ppermute | solution.py:18
  80.6 4.1 %collective-permute-start.7 = (f32[6,128,256]{2,1,0:T(8,128)S(1)}, f32[6,128,256]{2,1,0:T(8,128)S(1)}, u32[]{:S(2)}, u32[]{:S(2)}) collective-permute-start(f32[6,128,256]{2,1,0:T(8,128)S(1)} %dynamic-slice_select_fusion), channel_id=1, source_target_pairs={{4,0},{6,2},{8,4},{10,6},{12,8},{14,10},{16,12},{18,14},{20,16},{2... | collective-permute-start | bytes 2359304 | tf_op jit(solution)/shard_map/ppermute | solution.py:18
  86.7 2.0 %collective-permute-start.4 = (f32[6,128,256]{2,1,0:T(8,128)S(1)}, f32[6,128,256]{2,1,0:T(8,128)S(1)}, u32[]{:S(2)}, u32[]{:S(2)}) collective-permute-start(f32[6,128,256]{2,1,0:T(8,128)S(1)} %dynamic-slice_select_fusion), channel_id=1, source_target_pairs={{0,4},{2,6},{4,8},{6,10},{8,12},{10,14},{12,16},{14,18},{16,20},{1... | collective-permute-start | bytes 2359304 | tf_op jit(solution)/shard_map/ppermute | solution.py:18
  88.6 5.3 %collective-permute-start.6 = (f32[6,128,256]{2,1,0:T(8,128)S(1)}, f32[6,128,256]{2,1,0:T(8,128)S(1)}, u32[]{:S(2)}, u32[]{:S(2)}) collective-permute-start(f32[6,128,256]{2,1,0:T(8,128)S(1)} %dynamic-slice_select_fusion), channel_id=1, source_target_pairs={{2,0},{4,2},{6,4},{8,6},{10,8},{12,10},{14,12},{16,14},{18,16},{20... | collective-permute-start | bytes 2359304 | tf_op jit(solution)/shard_map/ppermute | solution.py:18
  95.0 11.3 %collective-permute-done.5 = f32[6,128,256]{2,1,0:T(8,128)S(1)} collective-permute-done((f32[6,128,256]{2,1,0:T(8,128)S(1)}, f32[6,128,256]{2,1,0:T(8,128)S(1)}, u32[]{:S(2)}, u32[]{:S(2)}) %collective-permute-start.5) | collective-permute-done | bytes 786464 | tf_op jit(solution)/shard_map/ppermute | solution.py:18
  107.3 27.2 %collective-permute-done.7 = f32[6,128,256]{2,1,0:T(8,128)S(1)} collective-permute-done((f32[6,128,256]{2,1,0:T(8,128)S(1)}, f32[6,128,256]{2,1,0:T(8,128)S(1)}, u32[]{:S(2)}, u32[]{:S(2)}) %collective-permute-start.7) | collective-permute-done | bytes 786464 | tf_op jit(solution)/shard_map/ppermute | solution.py:18
  135.5 1.1 fusion.10
  136.7 1.9 %fusion.11 = f32[4,128,256]{2,0,1:T(4,128)} fusion(f32[4,128,256]{2,0,1:T(4,128)S(1)} %fusion.12, f32[4,128,256]{2,0,1:T(4,128)S(1)} %fusion.10, f32[6,128,256]{2,1,0:T(8,128)S(1)} %collective-permute-done.6, s32[6]{0:T(128)S(1)} %iota_add_fusion.1, pred[6]{0:T(512)(128)(4,1)S(1)} %iota_compare_fusion.2, pred[]{:T(512)S(6)} %and.232, ...), kind=kOutput, calls=%fused_computation.17 | convolution fusion | flops 9699424 | bytes 2359347 | tf_op jit(solution)/shard_map/js,jab->sab/dot_general | solution.py:137
  138.6 12.2 %all-gather.2.cloned.1.call-done = f32[4,256,256]{2,0,1:T(4,128)} async-done(((f32[4,128,256]{2,0,1:T(4,128)}), f32[4,256,256]{2,0,1:T(4,128)}) %all-gather.2.cloned.1.call-update) | async-done | bytes 1048592 | tf_op jit(solution)/shard_map/all_gather | solution.py:140
  150.8 2.4 %copy.59 = f32[4,256,256]{2,1,0:T(8,128)} copy(f32[4,256,256]{2,0,1:T(4,128)} %all-gather.2.cloned.1.call-done) | data formatting | bytes 2097152
  (68 shorter events, 24.8 us)
Async XLA Ops:
  7.2 60.4 %copy-start = (f32[6,256,256]{2,1,0:T(8,128)S(1)}, f32[6,256,256]{2,1,0:T(8,128)}, u32[]{:S(2)}) copy-start(f32[6,256,256]{2,1,0:T(8,128)} %param.11) | copy-start | bytes 4718596
  7.2 12.8 %copy-start.6 = (u32[32]{0:T(128)S(1)}, u32[32]{0:T(128)}, u32[]{:S(2)}) copy-start(u32[32]{0:T(128)} %constant.69) | copy-start | bytes 388
  7.2 2.5 %copy-start.5 = (s32[48]{0:T(128)S(1)}, s32[48]{0:T(128)}, u32[]{:S(2)}) copy-start(s32[48]{0:T(128)} %param.13) | copy-start | bytes 580
  7.2 4.8 %copy-start.4 = (s32[16]{0:T(128)S(1)}, s32[16]{0:T(128)}, u32[]{:S(2)}) copy-start(s32[16]{0:T(128)} %param.12) | copy-start | bytes 196
  7.2 24.1 %all-reduce.3.cloned.1.call-start = ((), (), s32[]{:S(2)}) async-start(), calls=%async_computation.1 | async-start | bytes 1048576
  9.6 141.2 %all-gather.2.cloned.1.call-start = ((), (), s32[]{:S(2)}) async-start(), calls=%async_computation | async-start | bytes 1572864 | tf_op jit(solution)/shard_map/all_gather | solution.py:140
  32.4 12.3 %collective-permute-start.1 = (bf16[4,128,256]{2,0,1:T(4,128)(2,1)S(1)}, bf16[4,128,256]{2,0,1:T(4,128)(2,1)S(1)}, u32[]{:S(2)}, u32[]{:S(2)}) collective-permute-start(bf16[4,128,256]{2,0,1:T(4,128)(2,1)S(1)} %constant_dynamic-slice_fusion), channel_id=1, source_target_pairs={{2,0},{4,2},{6,4},{8,6},{10,8},{12,10},{14,12},{16,14},{18,16},{20... | collective-permute-start | bytes 786440 | tf_op jit(solution)/shard_map/ppermute | solution.py:18
  37.1 20.5 %collective-permute-start = (bf16[4,128,256]{2,0,1:T(4,128)(2,1)S(1)}, bf16[4,128,256]{2,0,1:T(4,128)(2,1)S(1)}, u32[]{:S(2)}, u32[]{:S(2)}) collective-permute-start(bf16[4,128,256]{2,0,1:T(4,128)(2,1)S(1)} %constant_dynamic-slice_fusion), channel_id=1, source_target_pairs={{4,0},{6,2},{8,4},{10,6},{12,8},{14,10},{16,12},{18,14},{20,16},{2... | collective-permute-start | bytes 786440 | tf_op jit(solution)/shard_map/ppermute | solution.py:18
  39.2 19.4 %collective-permute-start.3 = (bf16[4,128,256]{2,0,1:T(4,128)(2,1)S(1)}, bf16[4,128,256]{2,0,1:T(4,128)(2,1)S(1)}, u32[]{:S(2)}, u32[]{:S(2)}) collective-permute-start(bf16[4,128,256]{2,0,1:T(4,128)(2,1)S(1)} %constant_dynamic-slice_fusion), channel_id=1, source_target_pairs={{0,4},{2,6},{4,8},{6,10},{8,12},{10,14},{12,16},{14,18},{16,20},{1... | collective-permute-start | bytes 786440 | tf_op jit(solution)/shard_map/ppermute | solution.py:18
  42.4 16.7 %collective-permute-start.2 = (bf16[4,128,256]{2,0,1:T(4,128)(2,1)S(1)}, bf16[4,128,256]{2,0,1:T(4,128)(2,1)S(1)}, u32[]{:S(2)}, u32[]{:S(2)}) collective-permute-start(bf16[4,128,256]{2,0,1:T(4,128)(2,1)S(1)} %constant_dynamic-slice_fusion), channel_id=1, source_target_pairs={{0,2},{2,4},{4,6},{6,8},{8,10},{10,12},{12,14},{14,16},{16,18},{18... | collective-permute-start | bytes 786440 | tf_op jit(solution)/shard_map/ppermute | solution.py:18
  59.5 3.9 %copy-start.1 = (f32[6,256,256]{2,1,0:T(8,128)S(1)}, f32[6,256,256]{2,1,0:T(8,128)}, u32[]{:S(2)}) copy-start(f32[6,256,256]{2,1,0:T(8,128)} %param.10) | copy-start | bytes 4718596
  63.4 1.5 copy-start.2
  67.6 1.7 %copy-start.3 = (f32[6,256,256]{2,1,0:T(8,128)S(1)}, f32[6,256,256]{2,1,0:T(8,128)}, u32[]{:S(2)}) copy-start(f32[6,256,256]{2,1,0:T(8,128)} %param.9) | copy-start | bytes 4718596
  77.6 28.7 %collective-permute-start.5 = (f32[6,128,256]{2,1,0:T(8,128)S(1)}, f32[6,128,256]{2,1,0:T(8,128)S(1)}, u32[]{:S(2)}, u32[]{:S(2)}) collective-permute-start(f32[6,128,256]{2,1,0:T(8,128)S(1)} %dynamic-slice_select_fusion), channel_id=1, source_target_pairs={{0,2},{2,4},{4,6},{6,8},{8,10},{10,12},{12,14},{14,16},{16,18},{18... | collective-permute-start | bytes 2359304 | tf_op jit(solution)/shard_map/ppermute | solution.py:18
  80.6 53.9 %collective-permute-start.7 = (f32[6,128,256]{2,1,0:T(8,128)S(1)}, f32[6,128,256]{2,1,0:T(8,128)S(1)}, u32[]{:S(2)}, u32[]{:S(2)}) collective-permute-start(f32[6,128,256]{2,1,0:T(8,128)S(1)} %dynamic-slice_select_fusion), channel_id=1, source_target_pairs={{4,0},{6,2},{8,4},{10,6},{12,8},{14,10},{16,12},{18,14},{20,16},{2... | collective-permute-start | bytes 2359304 | tf_op jit(solution)/shard_map/ppermute | solution.py:18
  86.7 48.9 %collective-permute-start.4 = (f32[6,128,256]{2,1,0:T(8,128)S(1)}, f32[6,128,256]{2,1,0:T(8,128)S(1)}, u32[]{:S(2)}, u32[]{:S(2)}) collective-permute-start(f32[6,128,256]{2,1,0:T(8,128)S(1)} %dynamic-slice_select_fusion), channel_id=1, source_target_pairs={{0,4},{2,6},{4,8},{6,10},{8,12},{10,14},{12,16},{14,18},{16,20},{1... | collective-permute-start | bytes 2359304 | tf_op jit(solution)/shard_map/ppermute | solution.py:18
  88.6 48.0 %collective-permute-start.6 = (f32[6,128,256]{2,1,0:T(8,128)S(1)}, f32[6,128,256]{2,1,0:T(8,128)S(1)}, u32[]{:S(2)}, u32[]{:S(2)}) collective-permute-start(f32[6,128,256]{2,1,0:T(8,128)S(1)} %dynamic-slice_select_fusion), channel_id=1, source_target_pairs={{2,0},{4,2},{6,4},{8,6},{10,8},{12,10},{14,12},{16,14},{18,16},{20... | collective-permute-start | bytes 2359304 | tf_op jit(solution)/shard_map/ppermute | solution.py:18
Sparse Core Ops, SparseCore 0:
  10.9 20.3 all-reduce.2
  138.7 12.0 all-gather.1
where the time goes:
time: 162 us; the launch traced here: 160 us
  waiting for transfers between devices  70.7 us (44%)
  starting transfers between devices  24.5 us (15%)
  matrix products  22.2 us (14%)
  other arithmetic  15.5 us (10%)
  between operations  15.2 us (9%)
  local copies, waits for them, and re-layouts  8.05 us (5%)
  blocking collectives  3.77 us (2%)
    ppermute x8, waiting for transfers between devices, from_behind(): lax.ppermute(value, axis, [(source, source + steps) for source in range(i...  51.5 us
    ppermute x8, starting transfers between devices, from_behind(): lax.ppermute(value, axis, [(source, source + steps) for source in range(i...  24.4 us
    all_gather x1, waiting for transfers between devices, body(): direction = lax.all_gather(collected, 'dp', axis=1, tiled=True)  12.2 us
    unnamed x3, waiting for transfers between devices  7 us
    unnamed x18, local copies, waits for them, and re-layouts  6.41 us
    dot_general x5, matrix products, body(): jnp.einsum('js,jab->sab', matching.astype(jnp.float32), arriving, precisi...  6.12 us
    add x6, other arithmetic, linking(): holder_pos = hold_start + jnp.arange(slot_count, dtype=jnp.int32)  3.84 us
    all_gather x1, blocking collectives, body(): lax.all_gather(assembled.astype(jnp.bfloat16), 'dp', axis=1, tiled=True)  3.77 us
  transfers between devices with their start and end apart: 10, of which 6 were waited for; matrix products, arithmetic and copies ran while one was open for 15% of the time, Pallas kernels for 0%

commit v1 on v0

v1 whole, which is shorter than its diff:
```python
import functools

import jax
import jax.numpy as jnp
from jax import lax
from jax.experimental import pallas as pl
from jax.experimental.pallas import tpu as pltpu
from jax.sharding import PartitionSpec as P

REACH = 2
SIDES = 2 * REACH + 1
STEP = 10
LEVELS = 32767.0

beta_one = 0.9
beta_two = 0.95
epsilon = 1e-08

MESH = pl.DeviceIdType.MESH


def ring_barrier(me, devices, core):
    barrier = pltpu.get_barrier_semaphore()
    pl.semaphore_signal(barrier, inc=1, device_id={"dp": 1 - core}, device_id_type=MESH)
    for side in range(SIDES):
        if side == REACH:
            continue
        other = me + side - REACH

        @pl.when((other >= 0) & (other < devices))
        def _():
            pl.semaphore_signal(barrier, inc=1, device_id={"fsdp": other}, device_id_type=MESH)

    below = jnp.minimum(me, REACH)
    above = jnp.minimum(devices - 1 - me, REACH)
    pl.semaphore_wait(barrier, 1 + below + above)


def in_range(me, side, devices):
    other = me + side - REACH
    return (other >= 0) & (other < devices)


def gather_kernel(devices, slots, g_ref, out_ref, part, rs_send, rs_recv, send, recv, fsend, frecv):
    me = lax.axis_index("fsdp")
    core = lax.axis_index("dp")
    half = g_ref.shape[2] // 2
    mine = pl.ds(pl.multiple_of(core * half, half), half)
    theirs = pl.ds(pl.multiple_of((1 - core) * half, half), half)
    partner = {"dp": 1 - core}

    def reduce_copy(s):
        return pltpu.make_async_remote_copy(
            g_ref.at[0, s, theirs], part.at[s], rs_send.at[s], rs_recv.at[s], partner, MESH
        )

    def send_copy(side, s):
        return pltpu.make_async_remote_copy(
            out_ref.at[REACH * slots + s, mine],
            out_ref.at[(SIDES - 1 - side) * slots + s, mine],
            send.at[side * slots + s],
            recv.at[(SIDES - 1 - side) * slots + s],
            {"fsdp": me + side - REACH},
            MESH,
        )

    def arrival(side, s):
        at = side * slots + s
        return pltpu.make_async_remote_copy(
            out_ref.at[at, mine], out_ref.at[at, mine], send.at[at], recv.at[at], partner, MESH
        )

    def forward(side, s, rows):
        at = side * slots + s
        return pltpu.make_async_remote_copy(
            out_ref.at[at, rows], out_ref.at[at, rows], fsend.at[at], frecv.at[at], partner, MESH
        )

    ring_barrier(me, devices, core)
    for s in range(slots):
        reduce_copy(s).start()
    for s in range(slots):
        reduce_copy(s).wait_recv()
        total = g_ref[0, s, mine].astype(jnp.float32) + part[s].astype(jnp.float32)
        out_ref[REACH * slots + s, mine] = total.astype(jnp.bfloat16)
        for side in (0, 4, 1, 3):

            @pl.when(in_range(me, side, devices))
            def _():
                send_copy(side, s).start()

        forward(REACH, s, mine).start()
    for s in range(slots):
        for side in (0, 4, 1, 3):

            @pl.when(in_range(me, side, devices))
            def _():
                arrival(side, s).wait_recv()
                forward(side, s, mine).start()

    for s in range(slots):
        reduce_copy(s).wait_send()
        forward(REACH, s, mine).wait_send()
        forward(REACH, s, theirs).wait_recv()
        for side in (0, 4, 1, 3):

            @pl.when(in_range(me, side, devices))
            def _():
                send_copy(side, s).wait_send()
                forward(side, s, mine).wait_send()
                forward(side, s, theirs).wait_recv()


def return_kernel(
    devices, slots, q_ref, w_ref, out_ref, wout_ref,
    lsem, send, recv, fsend, frecv, wl, wsend, wrecv, wfsend, wfrecv,
):
    me = lax.axis_index("fsdp")
    core = lax.axis_index("dp")
    half = q_ref.shape[1]
    mine = pl.ds(pl.multiple_of(core * half, half), half)
    theirs = pl.ds(pl.multiple_of((1 - core) * half, half), half)
    partner = {"dp": 1 - core}

    def group(side):
        return pl.ds(side * slots, slots)

    def send_copy(side, s):
        return pltpu.make_async_remote_copy(
            q_ref.at[side * slots + s],
            out_ref.at[(SIDES - 1 - side) * slots + s, mine],
            send.at[side * slots + s],
            recv.at[(SIDES - 1 - side) * slots + s],
            {"fsdp": me + side - REACH},
            MESH,
        )

    def send_scale(side):
        return pltpu.make_async_remote_copy(
            w_ref.at[group(side)],
            wout_ref.at[core, group(SIDES - 1 - side)],
            wsend.at[side],
            wrecv.at[SIDES - 1 - side],
            {"fsdp": me + side - REACH},
            MESH,
        )

    def arrival(side, s):
        at = side * slots + s
        return pltpu.make_async_remote_copy(
            out_ref.at[at, mine], out_ref.at[at, mine], send.at[at], recv.at[at], partner, MESH
        )

    def arrival_scale(side):
        return pltpu.make_async_remote_copy(
            wout_ref.at[core, group(side)], wout_ref.at[core, group(side)],
            wsend.at[side], wrecv.at[side], partner, MESH,
        )

    def forward(side, s, rows):
        at = side * slots + s
        source = q_ref.at[at] if side == REACH else out_ref.at[at, rows]
        return pltpu.make_async_remote_copy(
            source, out_ref.at[at, rows], fsend.at[at], frecv.at[at], partner, MESH
        )

    def forward_scale(side, which):
        source = w_ref.at[group(side)] if side == REACH else wout_ref.at[which, group(side)]
        return pltpu.make_async_remote_copy(
            source, wout_ref.at[which, group(side)],
            wfsend.at[side], wfrecv.at[side], partner, MESH,
        )

    keep = [
        pltpu.make_async_copy(
            q_ref.at[REACH * slots + s], out_ref.at[REACH * slots + s, mine], lsem.at[s]
        )
        for s in range(slots)
    ]
    keep.append(
        pltpu.make_async_copy(w_ref.at[group(REACH)], wout_ref.at[core, group(REACH)], wl)
    )
    ring_barrier(me, devices, core)
    for side in (0, 4, 1, 3):

        @pl.when(in_range(me, side, devices))
        def _():
            send_scale(side).start()

    for s in range(slots):
        for side in (0, 4, 1, 3):

            @pl.when(in_range(me, side, devices))
            def _():
                send_copy(side, s).start()

    for s in range(slots):
        forward(REACH, s, mine).start()
    forward_scale(REACH, core).start()
    for copy in keep:
        copy.start()
    for side in (0, 4, 1, 3):

        @pl.when(in_range(me, side, devices))
        def _():
            arrival_scale(side).wait_recv()
            forward_scale(side, core).start()

    for s in range(slots):
        for side in (0, 4, 1, 3):

            @pl.when(in_range(me, side, devices))
            def _():
                arrival(side, s).wait_recv()
                forward(side, s, mine).start()

    for copy in keep:
        copy.wait()
    for side in range(SIDES):

        @pl.when(in_range(me, side, devices))
        def _():
            forward_scale(side, core).wait_send()
            forward_scale(side, 1 - core).wait_recv()
            if side != REACH:
                send_scale(side).wait_send()
            for s in range(slots):
                forward(side, s, mine).wait_send()
                forward(side, s, theirs).wait_recv()
                if side != REACH:
                    send_copy(side, s).wait_send()


def split(value):
    high = value.astype(jnp.bfloat16)
    low = (value - high.astype(jnp.float32)).astype(jnp.bfloat16)
    return high, low


def dot(a, b, dims=((1,), (0,))):
    return lax.dot_general(a, b, (dims, ((), ())), preferred_element_type=jnp.float32)


def step_kernel(place_ref, from_ref, live_ref, core_ref, g_ref, m_ref, v_ref, l_ref, r_ref,
                mo_ref, vo_ref, q_ref, w_ref):
    j = pl.program_id(0)
    half = q_ref.shape[1]
    width = g_ref.shape[2]
    live = live_ref[j] > 0

    @pl.when(live)
    def _():
        gradient = g_ref[0]
        moment = beta_one * m_ref[0] + (1.0 - beta_one) * gradient.astype(jnp.float32)
        mo_ref[0] = moment
        left_high, left_low = split(l_ref[0])
        right_high, right_low = split(r_ref[0])
        moment_high, moment_low = split(moment)
        first = ((0,), (0,))
        grad_side = dot(left_high, gradient, first) + dot(left_low, gradient, first)
        moment_side = (
            dot(left_high, moment_high, first)
            + dot(left_high, moment_low, first)
            + dot(left_low, moment_high, first)
        )
        both_high, both_low = split(jnp.concatenate([grad_side, moment_side], axis=0))
        turned = dot(both_high, right_high) + dot(both_high, right_low) + dot(both_low, right_high)
        turned_gradient = turned[:width]
        turned_moment = turned[width:]
        second = beta_two * v_ref[0] + (1.0 - beta_two) * turned_gradient * turned_gradient
        vo_ref[0] = second
        bias_one = 1.0 - beta_one**STEP
        bias_two = 1.0 - beta_two**STEP
        scaled = turned_moment / bias_one / (jnp.sqrt(second / bias_two) + epsilon)
        scaled_high, scaled_low = split(scaled)
        rows = pl.ds(pl.multiple_of(core_ref[0] * half, half), half)
        part_high, part_low = split(l_ref[0, rows])
        back = (
            dot(part_high, scaled_high) + dot(part_high, scaled_low) + dot(part_low, scaled_high)
        )
        back_high, back_low = split(back)
        last = ((1,), (1,))
        update = (
            dot(back_high, right_high, last)
            + dot(back_high, right_low, last)
            + dot(back_low, right_high, last)
        )
        peak = jnp.maximum(jnp.max(jnp.abs(update), axis=0, keepdims=True), 1e-30)
        q_ref[0] = jnp.round(update * (LEVELS / peak)).astype(jnp.int32).astype(jnp.int16)
        w_ref[0] = peak * (1.0 / LEVELS)

    @pl.when(jnp.logical_not(live))
    def _():
        mo_ref[...] = jnp.zeros_like(mo_ref)
        vo_ref[...] = jnp.zeros_like(vo_ref)
        q_ref[...] = jnp.zeros_like(q_ref)
        w_ref[...] = jnp.zeros_like(w_ref)


def place_kernel(from_ref, live_ref, q_ref, w_ref, d_ref):
    s = pl.program_id(0)
    half = q_ref.shape[1] // 2
    live = live_ref[s] > 0

    @pl.when(live)
    def _():
        for c in range(2):
            rows = pl.ds(c * half, half)
            d_ref[0, rows] = q_ref[0, rows].astype(jnp.int32).astype(jnp.float32) * w_ref[c, 0]

    @pl.when(jnp.logical_not(live))
    def _():
        d_ref[...] = jnp.zeros_like(d_ref)


def body(
    gradients, first_moment, second_moment, left_basis, right_basis, shard_starts, block_owners
):
    devices = lax.axis_size("fsdp")
    me = lax.axis_index("fsdp")
    core = lax.axis_index("dp")
    slots = gradients.shape[1]
    owned = first_moment.shape[0]
    width = gradients.shape[3]
    half = width // lax.axis_size("dp")
    blocks = block_owners.shape[0]
    places = SIDES * slots

    own_first = jnp.sum((block_owners < me).astype(jnp.int32))
    own_count = jnp.sum((block_owners == me).astype(jnp.int32))
    own_block = own_first + jnp.arange(owned, dtype=jnp.int32)
    passed = shard_starts[None, :] <= own_block[:, None]
    holder = jnp.sum(passed.astype(jnp.int32), axis=1) - 1
    holder_start = jnp.max(jnp.where(passed, shard_starts[None, :], 0), axis=1)
    own_live = (jnp.arange(owned) < own_count).astype(jnp.int32)
    spot = (holder - me + REACH) * slots + own_block - holder_start
    own_place = jnp.where(own_live > 0, spot, places)
    own_from = jnp.where(own_live > 0, spot, 0)

    starts = jnp.concatenate([shard_starts, jnp.full((1,), blocks, jnp.int32)])
    ids = jnp.arange(devices + 1)
    my_start = jnp.sum(jnp.where(ids == me, starts, 0))
    my_end = jnp.sum(jnp.where(ids == me + 1, starts, 0))
    slot_ids = jnp.arange(slots, dtype=jnp.int32)
    held_block = my_start + slot_ids
    held_live = (held_block < my_end).astype(jnp.int32)
    held_owner = jnp.sum(
        jnp.where(jnp.arange(blocks)[None, :] == held_block[:, None], block_owners[None, :], 0), axis=1
    )
    held_from = jnp.where(held_live > 0, (held_owner - me + REACH) * slots + slot_ids, 0)

    vmem = pl.BlockSpec(memory_space=pltpu.VMEM)
    dma = pltpu.SemaphoreType.DMA
    gathered = pl.pallas_call(
        functools.partial(gather_kernel, devices, slots),
        out_shape=jax.ShapeDtypeStruct((places, width, width), jnp.bfloat16),
        in_specs=[vmem],
        out_specs=vmem,
        scratch_shapes=[
            pltpu.VMEM((slots, half, width), jnp.bfloat16),
            dma((slots,)),
            dma((slots,)),
            dma((places,)),
            dma((places,)),
            dma((places,)),
            dma((places,)),
        ],
        compiler_params=pltpu.CompilerParams(collective_id=0, has_side_effects=True),
        name="gather",
    )(gradients)

    def by_own(j, place, origin, live, core):
        return (j, 0, 0)

    square = (1, width, width)
    moment_new, second_next, packed, scales = pl.pallas_call(
        step_kernel,
        grid_spec=pltpu.PrefetchScalarGridSpec(
            num_scalar_prefetch=4,
            grid=(owned,),
            in_specs=[
                pl.BlockSpec(square, lambda j, place, origin, live, core: (origin[j], 0, 0)),
                pl.BlockSpec(square, by_own),
                pl.BlockSpec(square, by_own),
                pl.BlockSpec(square, by_own),
                pl.BlockSpec(square, by_own),
            ],
            out_specs=[
                pl.BlockSpec(square, by_own),
                pl.BlockSpec(square, by_own),
                pl.BlockSpec((1, half, width), lambda j, place, origin, live, core: (place[j], 0, 0)),
                pl.BlockSpec((1, 1, width), lambda j, place, origin, live, core: (place[j], 0, 0)),
            ],
        ),
        out_shape=[
            jax.ShapeDtypeStruct(first_moment.shape, jnp.float32),
            jax.ShapeDtypeStruct(first_moment.shape, jnp.float32),
            jax.ShapeDtypeStruct((places + 1, half, width), jnp.int16),
            jax.ShapeDtypeStruct((places + 1, 1, width), jnp.float32),
        ],
        name="step",
    )(own_place, own_from, own_live, core[None].astype(jnp.int32),
      gathered, first_moment, second_moment, left_basis, right_basis)

    returned, return_scales = pl.pallas_call(
        functools.partial(return_kernel, devices, slots),
        out_shape=[
            jax.ShapeDtypeStruct((places, width, width), jnp.int16),
            jax.ShapeDtypeStruct((2, places, 1, width), jnp.float32),
        ],
        in_specs=[vmem, vmem],
        out_specs=[vmem, vmem],
        scratch_shapes=[
            dma((slots,)),
            dma((places,)),
            dma((places,)),
            dma((places,)),
            dma((places,)),
            dma,
            dma((SIDES,)),
            dma((SIDES,)),
            dma((SIDES,)),
            dma((SIDES,)),
        ],
        compiler_params=pltpu.CompilerParams(collective_id=1, has_side_effects=True),
        name="give_back",
    )(packed, scales)

    direction = pl.pallas_call(
        place_kernel,
        grid_spec=pltpu.PrefetchScalarGridSpec(
            num_scalar_prefetch=2,
            grid=(slots,),
            in_specs=[
                pl.BlockSpec(square, lambda s, origin, live: (origin[s], 0, 0)),
                pl.BlockSpec((2, 1, 1, width), lambda s, origin, live: (0, origin[s], 0, 0)),
            ],
            out_specs=pl.BlockSpec(square, lambda s, origin, live: (s, 0, 0)),
        ),
        out_shape=jax.ShapeDtypeStruct((slots, width, width), jnp.float32),
        name="place",
    )(held_from, held_live, returned, return_scales)
    return (direction, moment_new, second_next)


def solution(mesh):
    in_specs = (
        P("dp", "fsdp", None, None),
        P("fsdp", None, None),
        P("fsdp", None, None),
        P("fsdp", None, None),
        P("fsdp", None, None),
        P(),
        P(),
    )
    out_specs = (P("fsdp", None, None), P("fsdp", None, None), P("fsdp", None, None))
    return jax.shard_map(body, mesh=mesh, in_specs=in_specs, out_specs=out_specs, check_vma=False)
```

time: 162 us -> 79.7 us (0.49)
  waiting for transfers between devices: 70.7 us -> 0 us
  Pallas kernels: 0 us -> 67.2 us
  starting transfers between devices: 24.5 us -> 0 us
  matrix products: 22.2 us -> 0 us
  between operations: 15.2 us -> 0.71 us
  local copies, waits for them, and re-layouts: 8.05 us -> 0.01 us
  other arithmetic: 15.5 us -> 10.4 us
  blocking collectives: 3.77 us -> 0 us
    pallas_call x0 -> x4, Pallas kernels: none -> 67.2 us  [the longest x1 26.5 us: body(): pl.pallas_call(functools.partial(gather_kernel, devices, slots), out_shap...]
    ppermute x8 -> x0, waiting for transfers between devices: 51.5 us -> none  [from_behind(): lax.ppermute(value, axis, [(source, source + steps) for source in range(i...]
    ppermute x8 -> x0, starting transfers between devices: 24.4 us -> none  [from_behind(): lax.ppermute(value, axis, [(source, source + steps) for source in range(i...]
    dot_general x16 -> x0, matrix products: 22.2 us -> none  [the longest x5 6.12 us: body(): jnp.einsum('js,jab->sab', matching.astype(jnp.float32), arriving, precisi...]
    all_gather x1 -> x0, waiting for transfers between devices: 12.2 us -> none  [body(): direction = lax.all_gather(collected, 'dp', axis=1, tiled=True)]
    lt x12 -> x0, other arithmetic: 7.56 us -> none  [the longest x6 3.76 us: linking(): jnp.arange(slot_count)[None, :] < hold_count]
    unnamed x3 -> x0, waiting for transfers between devices: 7 us -> none
    unnamed x18 -> x4, local copies, waits for them, and re-layouts: 6.41 us -> 0.01 us
  transfers between devices with their start and end apart: 10 -> 0, of which waited for: 6 -> 0; matrix products, arithmetic and copies ran while one was open for 15% -> 0% of each run, Pallas kernels for 0% -> 0%
where the time goes in v1:
time: 79.7 us; the launch traced here: 78.4 us
  Pallas kernels  67.2 us (84%)
  other arithmetic  10.4 us (13%)
    pallas_call x1, Pallas kernels, body(): pl.pallas_call(functools.partial(gather_kernel, devices, slots), out_shap...  26.5 us
    pallas_call x1, Pallas kernels, body(): pl.pallas_call(functools.partial(return_kernel, devices, slots), out_shap...  25 us
    pallas_call x1, Pallas kernels, body(): pl.pallas_call(step_kernel, grid_spec=pltpu.PrefetchScalarGridSpec(num_sc...  11.7 us
    pallas_call x1, Pallas kernels, body(): pl.pallas_call(place_kernel, grid_spec=pltpu.PrefetchScalarGridSpec(num_s...  3.98 us
    select_n x1, other arithmetic, body(): own_from = jnp.where(own_live > 0, spot, 0)  1.81 us
    select_n x1, other arithmetic, body(): jnp.where(held_live > 0, (held_owner - me + REACH) * slots + slot_ids, 0)  1.79 us

profile of v1, /device:TPU:17, one launch (start us, length us, event | category | flops | bytes accessed | tf_op | source)
XLA Modules:
  0.0 78.4 jit_solution(5723498897119790281)
XLA Ops:
  0.6 1.3 %fusion.4 = (s32[]{:T(128)}, s32[]{:T(128)}) fusion(s32[48]{0:T(128)} %param.13, s32[]{:T(128)S(6)} %axis_index.23), kind=kLoop, calls=%fused_computation.17 | loop fusion | flops 286 | bytes 204 | tf_op jit(solution)/shard_map/reduce_sum | solution.py:330
  1.9 0.6 iota_add_fusion
  2.6 0.9 %fusion = (s32[6]{0:T(128)S(1)}, s32[6]{0:T(128)S(1)}) fusion(s32[16]{0:T(128)} %param.12, s32[6]{0:T(128)S(1)} %iota_add_fusion), kind=kLoop, calls=%fused_computation.2 | loop fusion | flops 468 | bytes 136 | tf_op jit(solution)/shard_map/reduce_sum | solution.py:333
  3.5 1.8 %compare_select_fusion.4 = (s32[6]{0:T(128)}, s32[6]{0:T(128)S(1)}) fusion(s32[]{:T(128)} %get-tuple-element.17, s32[6]{0:T(128)S(1)} %get-tuple-element.16, s32[]{:T(128)} %get-tuple-element.18, s32[]{:T(128)S(6)} %axis_index.23, s32[6]{0:T(128)S(1)} %get-tuple-element.15), kind=kLoop, calls=%fused_computation.13 | loop fusion | flops 66 | bytes 108 | tf_op jit(solution)/shard_map/jit(_where)/select_n | solution.py:338
  5.3 1.2 %compare_select_fusion.5.place_ref = s32[6]{0:T(128)} fusion(s32[6]{0:T(128)S(1)} %get-tuple-element.22, s32[]{:T(128)} %get-tuple-element.17), kind=kLoop, calls=%fused_computation.14 | loop fusion | flops 24 | bytes 52 | tf_op jit(solution)/shard_map/jit(_where)/select_n | solution.py:337
  6.5 1.2 %compare_convert_fusion.2.live_ref = s32[6]{0:T(128)} fusion(s32[]{:T(128)} %get-tuple-element.17), kind=kLoop, calls=%fused_computation.7 | loop fusion | flops 12 | bytes 28 | tf_op jit(solution)/shard_map/convert_element_type | solution.py:335
  7.7 26.5 %gather.1.g_ref = bf16[20,256,256]{2,1,0:T(8,128)(2,1)} custom-call(bf16[1,4,256,256]{3,2,1,0:T(8,128)(2,1)} %g_ref.1), custom_call_target="tpu_custom_call" | custom-call | tf_op jit(solution)/shard_map/gather/pallas_call | solution.py:354
  34.3 0.0 copy-start
  34.3 0.0 copy-start.1
  34.3 11.7 %step.1 = (f32[6,256,256]{2,1,0:T(8,128)}, f32[6,256,256]{2,1,0:T(8,128)}, s16[21,128,256]{2,1,0:T(8,128)(2,1)}, f32[21,1,256]{2,1,0:T(1,128)}) custom-call(s32[6]{0:T(128)} %compare_select_fusion.5.place_ref, s32[6]{0:T(128)} %get-tuple-element.21.from_ref, s32[6]{0:T(128)} %compare_convert_fusion.2.live_ref, s32[1]{0:T(128)} %bitcast.core_ref, ...), custom_call_target="tpu_custom_call" | custom-call | tf_op jit(solution)/shard_map/step/pallas_call | solution.py:376
  46.0 25.0 %give_back.1 = (s16[20,256,256]{2,1,0:T(8,128)(2,1)}, f32[2,20,1,256]{3,2,1,0:T(1,128)}) custom-call(s16[21,128,256]{2,1,0:T(8,128)(2,1)} %get-tuple-element.9.q_ref, f32[21,1,256]{2,1,0:T(1,128)} %get-tuple-element.10.w_ref), custom_call_target="tpu_custom_call" | custom-call | tf_op jit(solution)/shard_map/give_back/pallas_call | solution.py:405
  71.0 0.0 copy-done
  71.0 0.7 fusion.2
  71.7 0.6 iota_add_fusion.1
  72.4 0.0 copy-done.1
  72.4 0.2 select_reduce_fusion
  72.6 1.8 %compare_select_fusion.1 = (s32[4]{0:T(128)}, s32[4]{0:T(128)}) fusion(s32[4]{0:T(128)S(1)} %select_reduce_fusion, s32[]{:T(128)S(6)} %axis_index.23, s32[]{:T(128)} %get-tuple-element.20, s32[]{:T(128)} %get-tuple-element.19), kind=kLoop, calls=%fused_computation.9 | loop fusion | flops 36 | bytes 60 | tf_op jit(solution)/shard_map/jit(_where)/select_n | solution.py:350
  74.4 4.0 %place.1 = f32[4,256,256]{2,1,0:T(8,128)} custom-call(s32[4]{0:T(128)} %get-tuple-element.23.from_ref, s32[4]{0:T(128)} %get-tuple-element.24.live_ref, s16[20,256,256]{2,1,0:T(8,128)(2,1)} %get-tuple-element.11.q_ref, f32[2,20,1,256]{3,2,1,0:T(1,128)} %get-tuple-element.12.w_ref), custom_call_target="tpu_custom_call" | custom-call | tf_op jit(solution)/shard_map/place/pallas_call | solution.py:429
Async XLA Ops:
  34.3 36.7 %copy-start = (s32[16]{0:T(128)S(1)}, s32[16]{0:T(128)}, u32[]{:S(2)}) copy-start(s32[16]{0:T(128)} %param.12) | copy-start | bytes 196
  34.3 38.1 %copy-start.1 = (s32[48]{0:T(128)S(1)}, s32[48]{0:T(128)}, u32[]{:S(2)}) copy-start(s32[48]{0:T(128)} %param.13) | copy-start | bytes 580

commit v2 on v1

v2 whole, which is shorter than its diff:
```python
import functools

import jax
import jax.numpy as jnp
from jax import lax
from jax.experimental import pallas as pl
from jax.experimental.pallas import tpu as pltpu
from jax.sharding import PartitionSpec as P

REACH = 2
SIDES = 2 * REACH + 1
STEP = 10
LEVELS = 32767.0

beta_one = 0.9
beta_two = 0.95
epsilon = 1e-08

MESH = pl.DeviceIdType.MESH


DIRECT = ((1, 2), (-1, 2), (1, -2), (-1, -2))

ONWARD = (
    ({1: (2,), 2: (4,)}, {2: (4,), -2: (-1,)}, {-2: (-4,), 2: (1,)}, {-2: (-4,), -1: (-2,)}),
    (
        {2: (4, 1)},
        {-1: (-4,), 3: (2,), 2: (4,)},
        {-2: (-4,), 1: (4,), -3: (-2,)},
        {-2: (-1, -4)},
    ),
)

HOPS = (
    {1: 1, 2: 1, -2: 2, -1: 3},
    {-1: 1, 2: 1, 1: 2, -2: 2, 3: 2},
    {-2: 1, 1: 1, -1: 2, 2: 2, -3: 2},
    {-1: 1, -2: 1, 2: 2, 1: 3},
)


def guarded(condition, action):
    if condition is None:
        action()
    else:
        pl.when(condition)(action)


def greet(me, core, devices):
    barrier = pltpu.get_barrier_semaphore()
    x = jnp.where(me % 2 == 0, me + 1, me - 1)
    y = jnp.where(me % 4 < 2, me + 2, me - 2)
    pl.semaphore_signal(barrier, inc=1, device_id={"dp": 1 - core}, device_id_type=MESH)
    pl.semaphore_signal(barrier, inc=1, device_id={"fsdp": x}, device_id_type=MESH)
    pl.semaphore_signal(barrier, inc=1, device_id={"fsdp": y}, device_id_type=MESH)

    @pl.when(me >= 4)
    def _():
        pl.semaphore_signal(barrier, inc=1, device_id={"fsdp": me - 4}, device_id_type=MESH)

    @pl.when(me + 4 < devices)
    def _():
        pl.semaphore_signal(barrier, inc=1, device_id={"fsdp": me + 4}, device_id_type=MESH)

    return barrier


def met(barrier, me, devices):
    outer = jnp.where(me >= 4, 1, 0) + jnp.where(me + 4 < devices, 1, 0)
    pl.semaphore_wait(barrier, 3 + outer)


def relay(me, place, core, devices, items, own, ready, land, osend, fsend, recv, dsend, drecv):
    partner = {"dp": 1 - core}
    below, above = me >= 4, me + 4 < devices

    def reach(step):
        to = place + step
        return below if to < 0 else above if to > 3 else None

    def own_copy(way, i):
        hop = DIRECT[place][way]
        return pltpu.make_async_remote_copy(
            own(i), land(-hop, i, core), osend.at[way * items + i],
            recv.at[(3 - hop) * items + i], {"fsdp": me + hop}, MESH,
        )

    routes = [(off, hop) for off, hops in ONWARD[core][place].items() for hop in hops]

    def onward(off, hop, i):
        return pltpu.make_async_remote_copy(
            land(off, i, core), land(off - hop, i, core),
            fsend.at[routes.index((off, hop)) * items + i],
            recv.at[(off - hop + 3) * items + i], {"fsdp": me + hop}, MESH,
        )

    def arrival(off, i):
        at = recv.at[(off + 3) * items + i]
        ref = land(off, i, core)
        return pltpu.make_async_remote_copy(ref, ref, at, at, partner, MESH)

    def across(off, i, which):
        at = (off + REACH) * items + i
        source = own(i) if off == 0 else land(off, i, which)
        return pltpu.make_async_remote_copy(
            source, land(off, i, which), dsend.at[at], drecv.at[at], partner, MESH
        )

    offsets = [off for off in HOPS[place] if abs(off) <= REACH or off in ONWARD[core][place]]
    for i in range(items):
        ready(i)
        for way in range(2):
            own_copy(way, i).start()
        across(0, i, core).start()
    order = sorted((i + 2 * (HOPS[place][off] - 1), off, i) for off in offsets for i in range(items))
    for _, off, i in order:

        def arrive(off=off, i=i):
            arrival(off, i).wait_recv()
            for hop in ONWARD[core][place].get(off, ()):
                guarded(reach(hop), lambda hop=hop: onward(off, hop, i).start())
            if abs(off) <= REACH:
                across(off, i, core).start()

        guarded(reach(off), arrive)
    for i in range(items):
        for way in range(2):
            own_copy(way, i).wait_send()
        across(0, i, core).wait_send()
        across(0, i, 1 - core).wait_recv()
    for off in offsets:

        def finish(off=off):
            for i in range(items):
                for hop in ONWARD[core][place].get(off, ()):
                    guarded(reach(hop), lambda hop=hop, i=i: onward(off, hop, i).wait_send())
                if abs(off) <= REACH:
                    across(off, i, core).wait_send()
                    across(off, i, 1 - core).wait_recv()

        guarded(reach(off), finish)


def tables(me, devices, slots, owned, starts_ref, owners_ref, table_ref):
    blocks = owners_ref.shape[0]
    start = starts_ref[me]
    end = jnp.where(me + 1 < devices, starts_ref[jnp.minimum(me + 1, devices - 1)], blocks)
    held_owner = [owners_ref[jnp.minimum(start + s, blocks - 1)] for s in range(slots)]

    def count(b, carry):
        owner = owners_ref[b]
        below, mine, *ahead = carry
        return (
            below + (owner < me).astype(jnp.int32),
            mine + (owner == me).astype(jnp.int32),
            *[n + (owner < held_owner[s]).astype(jnp.int32) for s, n in enumerate(ahead)],
        )

    zero = jnp.int32(0)
    first, mine, *ahead = lax.fori_loop(0, blocks, count, (zero,) * (2 + slots))

    def seek(i, carry):
        begin = starts_ref[i]
        found = []
        for j in range(owned):
            holder, at = carry[j]
            passed = begin <= first + j
            found.append(
                (jnp.where(passed, i, holder), jnp.where(passed, begin, at))
            )
        return tuple(found)

    found = lax.fori_loop(0, devices, seek, ((zero, zero),) * owned)
    for j in range(owned):
        holder, at = found[j]
        live = j < mine
        table_ref[j] = jnp.where(live, (holder - me + REACH) * slots + first + j - at, 0)
        table_ref[owned + j] = live.astype(jnp.int32)
    for s in range(slots):
        live = start + s < end
        spot = (held_owner[s] - me + REACH) * owned + start + s - ahead[s]
        table_ref[2 * owned + s] = jnp.where(live, spot, 0)
        table_ref[2 * owned + slots + s] = live.astype(jnp.int32)


def each_place(me, core, run):
    for place in range(4):
        for side in range(2):

            @pl.when((me % 4 == place) & (core == side))
            def _():
                run(place, side)


def gather_kernel(
    devices, slots, owned, starts_ref, owners_ref, g_ref, out_ref, table_ref,
    part, transit, rs_send, rs_recv, osend, fsend, recv, dsend, drecv,
):
    me = lax.axis_index("fsdp")
    core = lax.axis_index("dp")
    half = g_ref.shape[2] // 2
    barrier = greet(me, core, devices)
    tables(me, devices, slots, owned, starts_ref, owners_ref, table_ref)
    met(barrier, me, devices)

    def run(place, side):
        mine, theirs = pl.ds(side * half, half), pl.ds((1 - side) * half, half)

        def reduce_copy(s):
            return pltpu.make_async_remote_copy(
                g_ref.at[0, s, theirs], part.at[s], rs_send.at[s], rs_recv.at[s],
                {"dp": 1 - side}, MESH,
            )

        def ready(s):
            reduce_copy(s).wait_recv()
            total = g_ref[0, s, mine].astype(jnp.float32) + part[s].astype(jnp.float32)
            out_ref[REACH * slots + s, mine] = total.astype(jnp.bfloat16)

        def land(off, s, which):
            if abs(off) > REACH:
                return transit.at[s]
            return out_ref.at[(off + REACH) * slots + s, pl.ds(which * half, half)]

        for s in range(slots):
            reduce_copy(s).start()
        relay(me, place, side, devices, slots, lambda s: land(0, s, side), ready, land,
              osend, fsend, recv, dsend, drecv)
        for s in range(slots):
            reduce_copy(s).wait_send()

    each_place(me, core, run)


def return_kernel(
    devices, owned, q_ref, w_ref, out_ref, wout_ref,
    transit, wtransit, lsem, osend, fsend, recv, dsend, drecv,
):
    me = lax.axis_index("fsdp")
    core = lax.axis_index("dp")
    half = q_ref.shape[1]
    met(greet(me, core, devices), me, devices)

    def run(place, side):
        def own(i):
            return w_ref if i == 0 else q_ref.at[i - 1]

        def land(off, i, which):
            if i == 0:
                if abs(off) > REACH:
                    return wtransit
                return wout_ref.at[which, pl.ds((off + REACH) * owned, owned)]
            if abs(off) > REACH:
                return transit.at[i - 1]
            return out_ref.at[(off + REACH) * owned + i - 1, pl.ds(which * half, half)]

        def keep(i):
            return pltpu.make_async_copy(own(i), land(0, i, side), lsem.at[i])

        relay(me, place, side, devices, owned + 1, own, lambda i: keep(i).start(), land,
              osend, fsend, recv, dsend, drecv)
        for i in range(owned + 1):
            keep(i).wait()

    each_place(me, core, run)


def split(value):
    high = value.astype(jnp.bfloat16)
    low = (value - high.astype(jnp.float32)).astype(jnp.bfloat16)
    return high, low


def dot(a, b, dims=((1,), (0,))):
    return lax.dot_general(a, b, (dims, ((), ())), preferred_element_type=jnp.float32)


def step_kernel(table_ref, core_ref, g_ref, m_ref, v_ref, l_ref, r_ref,
                mo_ref, vo_ref, q_ref, w_ref):
    j = pl.program_id(0)
    half = q_ref.shape[1]
    width = g_ref.shape[2]
    live = table_ref[pl.num_programs(0) + j] > 0

    @pl.when(live)
    def _():
        gradient = g_ref[0]
        moment = beta_one * m_ref[0] + (1.0 - beta_one) * gradient.astype(jnp.float32)
        mo_ref[0] = moment
        left_high, left_low = split(l_ref[0])
        right_high, right_low = split(r_ref[0])
        moment_high, moment_low = split(moment)
        first = ((0,), (0,))
        grad_side = dot(left_high, gradient, first) + dot(left_low, gradient, first)
        moment_side = (
            dot(left_high, moment_high, first)
            + dot(left_high, moment_low, first)
            + dot(left_low, moment_high, first)
        )
        both_high, both_low = split(jnp.concatenate([grad_side, moment_side], axis=0))
        turned = dot(both_high, right_high) + dot(both_high, right_low) + dot(both_low, right_high)
        turned_gradient = turned[:width]
        turned_moment = turned[width:]
        second = beta_two * v_ref[0] + (1.0 - beta_two) * turned_gradient * turned_gradient
        vo_ref[0] = second
        bias_one = 1.0 - beta_one**STEP
        bias_two = 1.0 - beta_two**STEP
        scaled = turned_moment / bias_one / (jnp.sqrt(second / bias_two) + epsilon)
        scaled_high, scaled_low = split(scaled)
        rows = pl.ds(pl.multiple_of(core_ref[0] * half, half), half)
        part_high, part_low = split(l_ref[0, rows])
        back = (
            dot(part_high, scaled_high) + dot(part_high, scaled_low) + dot(part_low, scaled_high)
        )
        back_high, back_low = split(back)
        last = ((1,), (1,))
        update = (
            dot(back_high, right_high, last)
            + dot(back_high, right_low, last)
            + dot(back_low, right_high, last)
        )
        peak = jnp.maximum(jnp.max(jnp.abs(update), axis=0, keepdims=True), 1e-30)
        q_ref[0] = jnp.round(update * (LEVELS / peak)).astype(jnp.int32).astype(jnp.int16)
        w_ref[0] = peak * (1.0 / LEVELS)

    @pl.when(jnp.logical_not(live))
    def _():
        mo_ref[...] = jnp.zeros_like(mo_ref)
        vo_ref[...] = jnp.zeros_like(vo_ref)
        q_ref[...] = jnp.zeros_like(q_ref)
        w_ref[...] = jnp.zeros_like(w_ref)


def place_kernel(first, table_ref, q_ref, w_ref, d_ref):
    s = pl.program_id(0)
    half = q_ref.shape[1] // 2
    live = table_ref[first + pl.num_programs(0) + s] > 0

    @pl.when(live)
    def _():
        for c in range(2):
            rows = pl.ds(c * half, half)
            d_ref[0, rows] = q_ref[0, rows].astype(jnp.int32).astype(jnp.float32) * w_ref[c, 0]

    @pl.when(jnp.logical_not(live))
    def _():
        d_ref[...] = jnp.zeros_like(d_ref)


def body(
    gradients, first_moment, second_moment, left_basis, right_basis, shard_starts, block_owners
):
    devices = lax.axis_size("fsdp")
    me = lax.axis_index("fsdp")
    core = lax.axis_index("dp")
    slots = gradients.shape[1]
    owned = first_moment.shape[0]
    width = gradients.shape[3]
    half = width // lax.axis_size("dp")
    places = SIDES * slots

    vmem = pl.BlockSpec(memory_space=pltpu.VMEM)
    dma = pltpu.SemaphoreType.DMA
    smem = pl.BlockSpec(memory_space=pltpu.SMEM)
    gathered, table = pl.pallas_call(
        functools.partial(gather_kernel, devices, slots, owned),
        out_shape=[
            jax.ShapeDtypeStruct((places, width, width), jnp.bfloat16),
            jax.ShapeDtypeStruct((2 * (owned + slots),), jnp.int32),
        ],
        in_specs=[smem, smem, vmem],
        out_specs=[vmem, smem],
        scratch_shapes=[
            pltpu.VMEM((slots, half, width), jnp.bfloat16),
            pltpu.VMEM((slots, half, width), jnp.bfloat16),
            dma((slots,)),
            dma((slots,)),
            dma((2 * slots,)),
            dma((3 * slots,)),
            dma((7 * slots,)),
            dma((SIDES * slots,)),
            dma((SIDES * slots,)),
        ],
        compiler_params=pltpu.CompilerParams(collective_id=0, has_side_effects=True),
        name="gather",
    )(shard_starts, block_owners, gradients)

    def by_own(j, table, core):
        return (j, 0, 0)

    square = (1, width, width)
    moment_new, second_next, packed, scales = pl.pallas_call(
        step_kernel,
        grid_spec=pltpu.PrefetchScalarGridSpec(
            num_scalar_prefetch=2,
            grid=(owned,),
            in_specs=[
                pl.BlockSpec(square, lambda j, table, core: (table[j], 0, 0)),
                pl.BlockSpec(square, by_own),
                pl.BlockSpec(square, by_own),
                pl.BlockSpec(square, by_own),
                pl.BlockSpec(square, by_own),
            ],
            out_specs=[
                pl.BlockSpec(square, by_own),
                pl.BlockSpec(square, by_own),
                pl.BlockSpec((1, half, width), by_own),
                pl.BlockSpec((1, 1, width), by_own),
            ],
        ),
        out_shape=[
            jax.ShapeDtypeStruct(first_moment.shape, jnp.float32),
            jax.ShapeDtypeStruct(first_moment.shape, jnp.float32),
            jax.ShapeDtypeStruct((owned, half, width), jnp.int16),
            jax.ShapeDtypeStruct((owned, 1, width), jnp.float32),
        ],
        name="step",
    )(table, core[None].astype(jnp.int32),
      gathered, first_moment, second_moment, left_basis, right_basis)

    items = owned + 1
    returned, return_scales = pl.pallas_call(
        functools.partial(return_kernel, devices, owned),
        out_shape=[
            jax.ShapeDtypeStruct((SIDES * owned, width, width), jnp.int16),
            jax.ShapeDtypeStruct((2, SIDES * owned, 1, width), jnp.float32),
        ],
        in_specs=[vmem, vmem],
        out_specs=[vmem, vmem],
        scratch_shapes=[
            pltpu.VMEM((owned, half, width), jnp.int16),
            pltpu.VMEM((owned, 1, width), jnp.float32),
            dma((items,)),
            dma((2 * items,)),
            dma((3 * items,)),
            dma((7 * items,)),
            dma((SIDES * items,)),
            dma((SIDES * items,)),
        ],
        compiler_params=pltpu.CompilerParams(collective_id=1, has_side_effects=True),
        name="give_back",
    )(packed, scales)

    base = 2 * owned
    direction = pl.pallas_call(
        functools.partial(place_kernel, base),
        grid_spec=pltpu.PrefetchScalarGridSpec(
            num_scalar_prefetch=1,
            grid=(slots,),
            in_specs=[
                pl.BlockSpec(square, lambda s, table: (table[base + s], 0, 0)),
                pl.BlockSpec((2, 1, 1, width), lambda s, table: (0, table[base + s], 0, 0)),
            ],
            out_specs=pl.BlockSpec(square, lambda s, table: (s, 0, 0)),
        ),
        out_shape=jax.ShapeDtypeStruct((slots, width, width), jnp.float32),
        name="place",
    )(table, returned, return_scales)
    return (direction, moment_new, second_next)


def solution(mesh):
    in_specs = (
        P("dp", "fsdp", None, None),
        P("fsdp", None, None),
        P("fsdp", None, None),
        P("fsdp", None, None),
        P("fsdp", None, None),
        P(),
        P(),
    )
    out_specs = (P("fsdp", None, None), P("fsdp", None, None), P("fsdp", None, None))
    return jax.shard_map(body, mesh=mesh, in_specs=in_specs, out_specs=out_specs, check_vma=False)
```

time: 79.7 us -> 68.8 us (0.86)
  other arithmetic: 10.4 us -> 0 us
    select_n x3 -> x0, other arithmetic: 4.82 us -> none  [the longest x1 1.81 us: body(): own_from = jnp.where(own_live > 0, spot, 0)]
    reduce_sum x4 -> x0, other arithmetic: 3.06 us -> none  [the longest x1 1.3 us: body(): own_count = jnp.sum((block_owners == me).astype(jnp.int32))]
    add x2 -> x0, other arithmetic: 1.29 us -> none  [the longest x1 0.65 us: body(): own_block = own_first + jnp.arange(owned, dtype=jnp.int32)]
    convert_element_type x1 -> x0, other arithmetic: 1.23 us -> none  [body(): own_live = (jnp.arange(owned) < own_count).astype(jnp.int32)]
where the time goes in v2:
time: 68.8 us; the launch traced here: 67.6 us
  Pallas kernels  67 us (97%)
    pallas_call x1, Pallas kernels, body(): pl.pallas_call(functools.partial(return_kernel, devices, owned), out_shap...  28.1 us
    pallas_call x1, Pallas kernels, body(): pl.pallas_call(functools.partial(gather_kernel, devices, slots, owned), o...  23.3 us
    pallas_call x1, Pallas kernels, body(): pl.pallas_call(step_kernel, grid_spec=pltpu.PrefetchScalarGridSpec(num_sc...  11.6 us
    pallas_call x1, Pallas kernels, body(): pl.pallas_call(functools.partial(place_kernel, base), grid_spec=pltpu.Pre...  3.97 us

profile of v2, /device:TPU:17, one launch (start us, length us, event | category | flops | bytes accessed | tf_op | source)
XLA Modules:
  0.0 67.6 jit_solution(9786376779497997344)
XLA Ops:
  0.6 23.3 %gather.1 = (bf16[20,256,256]{2,1,0:T(8,128)(2,1)}, s32[20]{0:T(128)}) custom-call(s32[16]{0:T(128)} %starts_ref.1, s32[48]{0:T(128)} %owners_ref.1, bf16[1,4,256,256]{3,2,1,0:T(8,128)(2,1)} %g_ref.1), custom_call_target="tpu_custom_call" | custom-call | tf_op jit(solution)/shard_map/gather/pallas_call | solution.py:365
  23.9 11.6 %step.1 = (f32[6,256,256]{2,1,0:T(8,128)}, f32[6,256,256]{2,1,0:T(8,128)}, s16[6,128,256]{2,1,0:T(8,128)(2,1)}, f32[6,1,256]{2,1,0:T(1,128)}) custom-call(s32[20]{0:T(128)} %get-tuple-element.11.table_ref, s32[1]{0:T(128)} %bitcast.core_ref, bf16[20,256,256]{2,1,0:T(8,128)(2,1)} %get-tuple-element.12.g_ref, f32[6,256,256]{2,1,0:T(8,128)} %m_ref.1, ...), custom_call_target="tpu_custom_call" | custom-call | tf_op jit(solution)/shard_map/step/pallas_call | solution.py:392
  35.5 28.1 %give_back.1 = (s16[30,256,256]{2,1,0:T(8,128)(2,1)}, f32[2,30,1,256]{3,2,1,0:T(1,128)}) custom-call(s16[6,128,256]{2,1,0:T(8,128)(2,1)} %get-tuple-element.13.q_ref, f32[6,1,256]{2,1,0:T(1,128)} %get-tuple-element.14.w_ref), custom_call_target="tpu_custom_call" | custom-call | tf_op jit(solution)/shard_map/give_back/pallas_call | solution.py:422
  63.7 4.0 %place.1 = f32[4,256,256]{2,1,0:T(8,128)} custom-call(s32[20]{0:T(128)} %get-tuple-element.11.table_ref, s16[30,256,256]{2,1,0:T(8,128)(2,1)} %get-tuple-element.15.q_ref, f32[2,30,1,256]{3,2,1,0:T(1,128)} %get-tuple-element.16.w_ref), custom_call_target="tpu_custom_call" | custom-call | tf_op jit(solution)/shard_map/place/pallas_call | solution.py:445

commit v3 on v2

--- a/solution.py
+++ b/solution.py
@@ -232,35 +232,153 @@
     each_place(me, core, run)
 
 
+def step_to(place, hop):
+    return place if abs(hop) == 4 else place + hop
+
+
+def upward(core, place, off):
+    if off in DIRECT[place]:
+        return off
+    for hop in (1, -1, 2, -2, 4, -4):
+        before = step_to(place, -hop)
+        if 0 <= before < 4 and hop in ONWARD[core][before].get(off + hop, ()):
+            return -hop
+    raise ValueError(off)
+
+
+def height(core, place, off):
+    onward = ONWARD[core][place].get(off, ())
+    return max((1 + height(core, step_to(place, hop), off - hop) for hop in onward), default=0)
+
+
+def members(core, place, off, at):
+    found = [at] if abs(off) <= REACH else []
+    for hop in ONWARD[core][place].get(off, ()):
+        found += members(core, step_to(place, hop), off - hop, at + hop)
+    return found
+
+
+def ports(core, place):
+    routes = [(off, hop) for off, hops in ONWARD[core][place].items() for hop in hops]
+    return [(0, hop) for hop in DIRECT[place]] + routes
+
+
 def return_kernel(
-    devices, owned, q_ref, w_ref, out_ref, wout_ref,
-    transit, wtransit, lsem, osend, fsend, recv, dsend, drecv,
+    devices, slots, starts_ref, owners_ref, q_ref, w_ref, out_ref,
+    arr_q, arr_w, pack_q, pack_w, send, recv, dsend, drecv,
 ):
     me = lax.axis_index("fsdp")
     core = lax.axis_index("dp")
-    half = q_ref.shape[1]
-    met(greet(me, core, devices), me, devices)
+    owned, half, _ = q_ref.shape
+    blocks = owners_ref.shape[0]
+    items = slots + 1
+    barrier = greet(me, core, devices)
+    first = lax.fori_loop(
+        0, blocks, lambda b, n: n + (owners_ref[b] < me).astype(jnp.int32), jnp.int32(0)
+    )
+    picks = {}
+    for off in range(-REACH, REACH + 1):
+        holder = jnp.clip(me + off, 0, devices - 1)
+        start = starts_ref[holder]
+        after = starts_ref[jnp.minimum(holder + 1, devices - 1)]
+        end = jnp.where(holder + 1 < devices, after, blocks)
+        for s in range(slots):
+            owner = owners_ref[jnp.minimum(start + s, blocks - 1)]
+            at = jnp.clip(start + s - first, 0, owned - 1)
+            picks[off, s] = (start + s < end, owner, at)
+    met(barrier, me, devices)
 
     def run(place, side):
-        def own(i):
-            return w_ref if i == 0 else q_ref.at[i - 1]
-
-        def land(off, i, which):
-            if i == 0:
-                if abs(off) > REACH:
-                    return wtransit
-                return wout_ref.at[which, pl.ds((off + REACH) * owned, owned)]
+        mine, theirs = pl.ds(side * half, half), pl.ds((1 - side) * half, half)
+        below, above = me >= 4, me + 4 < devices
+        gates = ports(side, place)
+        offsets = [off for off in HOPS[place] if abs(off) <= REACH or off in ONWARD[side][place]]
+
+        def reach(step):
+            to = place + step
+            return below if to < 0 else above if to > 3 else None
+
+        def inbox(port, i):
+            return arr_w.at[port] if i == 0 else arr_q.at[port, i - 1]
+
+        def send_copy(off, i):
+            node = offsets.index(off)
+            hop = upward(side, place, off)
+            port = ports(side, step_to(place, hop)).index((off - hop, -hop))
             if abs(off) > REACH:
-                return transit.at[i - 1]
-            return out_ref.at[(off + REACH) * owned + i - 1, pl.ds(which * half, half)]
-
-        def keep(i):
-            return pltpu.make_async_copy(own(i), land(0, i, side), lsem.at[i])
-
-        relay(me, place, side, devices, owned + 1, own, lambda i: keep(i).start(), land,
-              osend, fsend, recv, dsend, drecv)
-        for i in range(owned + 1):
-            keep(i).wait()
+                source = inbox(gates.index((off, ONWARD[side][place][off][0])), i)
+            else:
+                source = pack_w.at[node] if i == 0 else pack_q.at[node, i - 1]
+            return pltpu.make_async_remote_copy(
+                source, inbox(port, i), send.at[node * items + i], recv.at[port * items + i],
+                {"fsdp": me + hop}, MESH,
+            )
+
+        def arrival(port, i):
+            at = recv.at[port * items + i]
+            return pltpu.make_async_remote_copy(
+                inbox(port, i), inbox(port, i), at, at, {"dp": 1 - side}, MESH
+            )
+
+        def chosen(off, s, own_ref, arrived):
+            _, owner, at = picks[off, s]
+            value = own_ref[at]
+            onward = DIRECT[place] if off == 0 else ONWARD[side][place].get(off, ())
+            if onward:
+                came = arrived[gates.index((off, onward[-1])), s]
+                if len(onward) == 2:
+                    hop = onward[0]
+                    group = members(side, step_to(place, hop), off - hop, hop)
+                    inside = functools.reduce(jnp.logical_or, [owner == me + to for to in group])
+                    came = lax.select(inside, arrived[gates.index((off, hop)), s], came)
+                value = lax.select(owner == me, value, came)
+            return value
+
+        def collect(off, i):
+            onward = DIRECT[place] if off == 0 else ONWARD[side][place].get(off, ())
+            for hop in onward:
+                port = gates.index((off, hop))
+                guarded(reach(hop), lambda port=port: arrival(port, i).wait_recv())
+
+        def pass_on(off, i):
+            collect(off, i)
+            node = offsets.index(off)
+            if abs(off) <= REACH:
+                if i == 0:
+                    for s in range(slots):
+                        pack_w[node, s] = chosen(off, s, w_ref, arr_w)
+                else:
+                    pack_q[node, i - 1] = chosen(off, i - 1, q_ref, arr_q)
+            send_copy(off, i).start()
+
+        def across(s, rows):
+            return pltpu.make_async_remote_copy(
+                out_ref.at[s, rows], out_ref.at[s, rows], dsend.at[s], drecv.at[s],
+                {"dp": 1 - side}, MESH,
+            )
+
+        order = sorted(
+            (i + 2 * height(side, place, off), off, i) for off in offsets for i in range(items)
+        )
+        for _, off, i in order:
+            guarded(reach(off), lambda off=off, i=i: pass_on(off, i))
+        collect(0, 0)
+        for s in range(slots):
+            collect(0, s + 1)
+            value = chosen(0, s, q_ref, arr_q).astype(jnp.int32).astype(jnp.float32)
+            value = value * chosen(0, s, w_ref, arr_w)
+            out_ref[s, mine] = lax.select(picks[0, s][0], value, jnp.zeros_like(value))
+            across(s, mine).start()
+        for off in offsets:
+
+            def finish(off=off):
+                for i in range(items):
+                    send_copy(off, i).wait_send()
+
+            guarded(reach(off), finish)
+        for s in range(slots):
+            across(s, mine).wait_send()
+            across(s, theirs).wait_recv()
 
     each_place(me, core, run)
 
@@ -329,22 +447,6 @@
         vo_ref[...] = jnp.zeros_like(vo_ref)
         q_ref[...] = jnp.zeros_like(q_ref)
         w_ref[...] = jnp.zeros_like(w_ref)
-
-
-def place_kernel(first, table_ref, q_ref, w_ref, d_ref):
-    s = pl.program_id(0)
-    half = q_ref.shape[1] // 2
-    live = table_ref[first + pl.num_programs(0) + s] > 0
-
-    @pl.when(live)
-    def _():
-        for c in range(2):
-            rows = pl.ds(c * half, half)
-            d_ref[0, rows] = q_ref[0, rows].astype(jnp.int32).astype(jnp.float32) * w_ref[c, 0]
-
-    @pl.when(jnp.logical_not(live))
-    def _():
-        d_ref[...] = jnp.zeros_like(d_ref)
 
 
 def body(
@@ -418,44 +520,25 @@
     )(table, core[None].astype(jnp.int32),
       gathered, first_moment, second_moment, left_basis, right_basis)
 
-    items = owned + 1
-    returned, return_scales = pl.pallas_call(
-        functools.partial(return_kernel, devices, owned),
-        out_shape=[
-            jax.ShapeDtypeStruct((SIDES * owned, width, width), jnp.int16),
-            jax.ShapeDtypeStruct((2, SIDES * owned, 1, width), jnp.float32),
-        ],
-        in_specs=[vmem, vmem],
-        out_specs=[vmem, vmem],
+    items = slots + 1
+    direction = pl.pallas_call(
+        functools.partial(return_kernel, devices, slots),
+        out_shape=jax.ShapeDtypeStruct((slots, width, width), jnp.float32),
+        in_specs=[smem, smem, vmem, vmem],
+        out_specs=vmem,
         scratch_shapes=[
-            pltpu.VMEM((owned, half, width), jnp.int16),
-            pltpu.VMEM((owned, 1, width), jnp.float32),
-            dma((items,)),
-            dma((2 * items,)),
-            dma((3 * items,)),
-            dma((7 * items,)),
-            dma((SIDES * items,)),
-            dma((SIDES * items,)),
+            pltpu.VMEM((5, slots, half, width), jnp.int16),
+            pltpu.VMEM((5, slots, 1, width), jnp.float32),
+            pltpu.VMEM((5, slots, half, width), jnp.int16),
+            pltpu.VMEM((5, slots, 1, width), jnp.float32),
+            dma((5 * items,)),
+            dma((5 * items,)),
+            dma((slots,)),
+            dma((slots,)),
         ],
         compiler_params=pltpu.CompilerParams(collective_id=1, has_side_effects=True),
         name="give_back",
-    )(packed, scales)
-
-    base = 2 * owned
-    direction = pl.pallas_call(
-        functools.partial(place_kernel, base),
-        grid_spec=pltpu.PrefetchScalarGridSpec(
-            num_scalar_prefetch=1,
-            grid=(slots,),
-            in_specs=[
-                pl.BlockSpec(square, lambda s, table: (table[base + s], 0, 0)),
-                pl.BlockSpec((2, 1, 1, width), lambda s, table: (0, table[base + s], 0, 0)),
-            ],
-            out_specs=pl.BlockSpec(square, lambda s, table: (s, 0, 0)),
-        ),
-        out_shape=jax.ShapeDtypeStruct((slots, width, width), jnp.float32),
-        name="place",
-    )(table, returned, return_scales)
+    )(shard_starts, block_owners, packed, scales)
     return (direction, moment_new, second_next)
 
 

time: 68.8 us -> 59.8 us (0.87); the launches traced: 67.6 us -> 59.5 us
  Pallas kernels: 67 us -> 56.6 us
  local copies, waits for them, and re-layouts: 0 us -> 2.29 us
    pallas_call x2 -> x1, Pallas kernels: 32.1 us -> 21.7 us  [body(): pl.pallas_call(functools.partial(return_kernel, devices, slots), out_shap...]
    unnamed x0 -> x1, local copies, waits for them, and re-layouts: none -> 2.29 us
where the time goes in v3:
time: 59.8 us; the launch traced here: 59.5 us
  Pallas kernels  56.6 us (95%)
  local copies, waits for them, and re-layouts  2.29 us (4%)
  between operations  0.65 us (1%)
    pallas_call x1, Pallas kernels, body(): pl.pallas_call(functools.partial(gather_kernel, devices, slots, owned), o...  23.3 us
    pallas_call x1, Pallas kernels, body(): pl.pallas_call(functools.partial(return_kernel, devices, slots), out_shap...  21.7 us
    pallas_call x1, Pallas kernels, body(): pl.pallas_call(step_kernel, grid_spec=pltpu.PrefetchScalarGridSpec(num_sc...  11.6 us
    unnamed x1, local copies, waits for them, and re-layouts  2.29 us

profile of v3, /device:TPU:17, one launch (start us, length us, event | category | flops | bytes accessed | tf_op | source)
XLA Modules:
  0.0 59.5 jit_solution(14652879245810355564)
XLA Ops:
  0.6 23.3 %gather.1 = (bf16[20,256,256]{2,1,0:T(8,128)(2,1)}, s32[20]{0:T(128)}) custom-call(s32[16]{0:T(128)} %starts_ref.3, s32[48]{0:T(128)} %owners_ref.3, bf16[1,4,256,256]{3,2,1,0:T(8,128)(2,1)} %g_ref.1), custom_call_target="tpu_custom_call" | custom-call | tf_op jit(solution)/shard_map/gather/pallas_call | solution.py:467
  23.9 11.6 %step.1 = (f32[6,256,256]{2,1,0:T(8,128)}, f32[6,256,256]{2,1,0:T(8,128)}, s16[6,128,256]{2,1,0:T(8,128)(2,1)}, f32[6,1,256]{2,1,0:T(1,128)}) custom-call(s32[20]{0:T(128)} %get-tuple-element.9.table_ref, s32[1]{0:T(128)} %bitcast.core_ref, bf16[20,256,256]{2,1,0:T(8,128)(2,1)} %get-tuple-element.10.g_ref, f32[6,256,256]{2,1,0:T(8,128)} %m_ref.1, ...), custom_call_target="tpu_custom_call" | custom-call | tf_op jit(solution)/shard_map/step/pallas_call | solution.py:494
  35.5 21.7 %give_back.1 = f32[4,256,256]{2,1,0:T(8,128)} custom-call(s32[16]{0:T(128)} %starts_ref.3, s32[48]{0:T(128)} %owners_ref.3, s16[6,128,256]{2,1,0:T(8,128)(2,1)} %get-tuple-element.11.q_ref, f32[6,1,256]{2,1,0:T(1,128)} %get-tuple-element.12.w_ref), custom_call_target="tpu_custom_call" | custom-call | tf_op jit(solution)/shard_map/give_back/pallas_call | solution.py:524
  57.2 2.3 %copy.11 = f32[4,256,256]{2,1,0:T(8,128)} copy(f32[4,256,256]{2,1,0:T(8,128)} %give_back.1) | data formatting | bytes 2097152

commit v4 on v3

--- a/solution.py
+++ b/solution.py
@@ -194,7 +194,7 @@
 
 def gather_kernel(
     devices, slots, owned, starts_ref, owners_ref, g_ref, out_ref, table_ref,
-    part, transit, rs_send, rs_recv, osend, fsend, recv, dsend, drecv,
+    landed, part, transit, rs_send, rs_recv, osend, fsend, recv, dsend, drecv,
 ):
     me = lax.axis_index("fsdp")
     core = lax.axis_index("dp")
@@ -215,12 +215,12 @@
         def ready(s):
             reduce_copy(s).wait_recv()
             total = g_ref[0, s, mine].astype(jnp.float32) + part[s].astype(jnp.float32)
-            out_ref[REACH * slots + s, mine] = total.astype(jnp.bfloat16)
+            landed[REACH * slots + s, mine] = total.astype(jnp.bfloat16)
 
         def land(off, s, which):
             if abs(off) > REACH:
                 return transit.at[s]
-            return out_ref.at[(off + REACH) * slots + s, pl.ds(which * half, half)]
+            return landed.at[(off + REACH) * slots + s, pl.ds(which * half, half)]
 
         for s in range(slots):
             reduce_copy(s).start()
@@ -230,6 +230,8 @@
             reduce_copy(s).wait_send()
 
     each_place(me, core, run)
+    for j in range(owned):
+        out_ref[j] = landed[jnp.clip(table_ref[j], 0, SIDES * slots - 1)]
 
 
 def step_to(place, hop):
@@ -405,16 +407,13 @@
         gradient = g_ref[0]
         moment = beta_one * m_ref[0] + (1.0 - beta_one) * gradient.astype(jnp.float32)
         mo_ref[0] = moment
-        left_high, left_low = split(l_ref[0])
+        turn_high, turn_low = split(l_ref[0].T)
         right_high, right_low = split(r_ref[0])
         moment_high, moment_low = split(moment)
-        first = ((0,), (0,))
-        grad_side = dot(left_high, gradient, first) + dot(left_low, gradient, first)
-        moment_side = (
-            dot(left_high, moment_high, first)
-            + dot(left_high, moment_low, first)
-            + dot(left_low, moment_high, first)
-        )
+        pair = jnp.concatenate([gradient, moment_high], axis=1)
+        sides = dot(turn_high, pair) + dot(turn_low, pair)
+        grad_side = sides[:, :width]
+        moment_side = sides[:, width:] + dot(turn_high, moment_low)
         both_high, both_low = split(jnp.concatenate([grad_side, moment_side], axis=0))
         turned = dot(both_high, right_high) + dot(both_high, right_low) + dot(both_low, right_high)
         turned_gradient = turned[:width]
@@ -467,12 +466,13 @@
     gathered, table = pl.pallas_call(
         functools.partial(gather_kernel, devices, slots, owned),
         out_shape=[
-            jax.ShapeDtypeStruct((places, width, width), jnp.bfloat16),
+            jax.ShapeDtypeStruct((owned, width, width), jnp.bfloat16),
             jax.ShapeDtypeStruct((2 * (owned + slots),), jnp.int32),
         ],
         in_specs=[smem, smem, vmem],
         out_specs=[vmem, smem],
         scratch_shapes=[
+            pltpu.VMEM((places, width, width), jnp.bfloat16),
             pltpu.VMEM((slots, half, width), jnp.bfloat16),
             pltpu.VMEM((slots, half, width), jnp.bfloat16),
             dma((slots,)),
@@ -497,7 +497,7 @@
             num_scalar_prefetch=2,
             grid=(owned,),
             in_specs=[
-                pl.BlockSpec(square, lambda j, table, core: (table[j], 0, 0)),
+                pl.BlockSpec(square, by_own),
                 pl.BlockSpec(square, by_own),
                 pl.BlockSpec(square, by_own),
                 pl.BlockSpec(square, by_own),

time: 59.8 us -> 59.1 us (0.988)
  Pallas kernels: 56.6 us -> 55.8 us
where the time goes in v4:
time: 59.1 us; the launch traced here: 58.8 us
  Pallas kernels  55.8 us (94%)
  local copies, waits for them, and re-layouts  2.29 us (4%)
  between operations  0.65 us (1%)
    pallas_call x1, Pallas kernels, body(): pl.pallas_call(functools.partial(gather_kernel, devices, slots, owned), o...  22.7 us
    pallas_call x1, Pallas kernels, body(): pl.pallas_call(functools.partial(return_kernel, devices, slots), out_shap...  21.7 us
    pallas_call x1, Pallas kernels, body(): pl.pallas_call(step_kernel, grid_spec=pltpu.PrefetchScalarGridSpec(num_sc...  11.4 us
    unnamed x1, local copies, waits for them, and re-layouts  2.29 us

profile of v4, /device:TPU:17, one launch (start us, length us, event | category | flops | bytes accessed | tf_op | source)
XLA Modules:
  0.0 58.8 jit_solution(2973194821721361322)
XLA Ops:
  0.6 22.7 %gather.1 = (bf16[6,256,256]{2,1,0:T(8,128)(2,1)}, s32[20]{0:T(128)}) custom-call(s32[16]{0:T(128)} %starts_ref.3, s32[48]{0:T(128)} %owners_ref.3, bf16[1,4,256,256]{3,2,1,0:T(8,128)(2,1)} %g_ref.1), custom_call_target="tpu_custom_call" | custom-call | tf_op jit(solution)/shard_map/gather/pallas_call | solution.py:466
  23.3 11.4 %step.1 = (f32[6,256,256]{2,1,0:T(8,128)}, f32[6,256,256]{2,1,0:T(8,128)}, s16[6,128,256]{2,1,0:T(8,128)(2,1)}, f32[6,1,256]{2,1,0:T(1,128)}) custom-call(s32[20]{0:T(128)} %get-tuple-element.9.table_ref, s32[1]{0:T(128)} %bitcast.core_ref, bf16[6,256,256]{2,1,0:T(8,128)(2,1)} %get-tuple-element.10.g_ref, f32[6,256,256]{2,1,0:T(8,128)} %m_ref.1, ...), custom_call_target="tpu_custom_call" | custom-call | tf_op jit(solution)/shard_map/step/pallas_call | solution.py:494
  34.8 21.7 %give_back.1 = f32[4,256,256]{2,1,0:T(8,128)} custom-call(s32[16]{0:T(128)} %starts_ref.3, s32[48]{0:T(128)} %owners_ref.3, s16[6,128,256]{2,1,0:T(8,128)(2,1)} %get-tuple-element.11.q_ref, f32[6,1,256]{2,1,0:T(1,128)} %get-tuple-element.12.w_ref), custom_call_target="tpu_custom_call" | custom-call | tf_op jit(solution)/shard_map/give_back/pallas_call | solution.py:524
  56.5 2.3 %copy.11 = f32[4,256,256]{2,1,0:T(8,128)} copy(f32[4,256,256]{2,1,0:T(8,128)} %give_back.1) | data formatting | bytes 2097152
